TPU v7x, 256 devices: a whole 4x4x8 slice. The times are simulated.
256 devices in a mesh: zero: 32 (over y, x, core), tp: 8 (over z).
Axes of the slice: x: 4, y: 4, z: 8, core: 2. Of those that a mesh axis runs over, the one named last changes fastest.
Arguments:
- weight_gate: bfloat16 [2560, 9728], P('zero', 'tp'), may hold values from -0.125 to 0.125
- low_gate: bfloat16 [2560, 16], P('zero'), may hold values from -0.125 to 0.125
- high_gate: bfloat16 [16, 9728], P(None, 'tp'), may hold values from -1.5 to 1.5
- weight_up: bfloat16 [2560, 9728], P('zero', 'tp'), may hold values from -0.125 to 0.125
- low_up: bfloat16 [2560, 16], P('zero'), may hold values from -0.125 to 0.125
- high_up: bfloat16 [16, 9728], P(None, 'tp'), may hold values from -1.5 to 1.5
- weight_down: bfloat16 [9728, 2560], P('tp', 'zero'), may hold values from -0.0625 to 0.0625
- low_down: bfloat16 [9728, 16], P('tp'), may hold values from -0.0625 to 0.0625
- high_down: bfloat16 [16, 2560], P(None, 'zero'), may hold values from -1.5 to 1.5
- norm_train: float32 [2560], P(('zero', 'tp')), may hold values from 0.25 to 1.75
- norm_step: float32 [2560], P(('zero', 'tp')), may hold values from -0.3 to 0.3
Outputs:
- ready_gate: bfloat16 [2560, 9728], P(None, 'tp')
- ready_up: bfloat16 [2560, 9728], P(None, 'tp')
- ready_down: bfloat16 [9728, 2560], P('tp')
- serve_norm: bfloat16 [2560], replicated
All inputs are finite; a program needn't handle non-finite values.
Results may differ from a plain program's by a relative error of at most 0.001.
Values may be sent and summed in bfloat16 or wider, within the bound.
No kernel may reach another device: no remote copies, remote signals or barrier semaphores. Data moves between devices by JAX's collectives and lax.ppermute only.
A program may use at most 128 MiB of HBM per device.

v0:
```python
import jax
import jax.numpy as jnp
from jax import lax
from jax.sharding import Mesh
from jax.sharding import PartitionSpec as P

ZERO = ("zero_0", "zero_1", "zero_2")
ZERO_TP = ("zero_0", "zero_1", "zero_2", "tp")
mix_rate = 0.5


def turned_gather(arrays, axis, dims):
    turned = [jnp.moveaxis(a, dim, 0) for a, dim in zip(arrays, dims)]
    widths = [t[0].size for t in turned]
    both = jnp.concatenate([t.reshape(-1, w) for t, w in zip(turned, widths)], axis=1)
    out = lax.all_gather(both, axis, axis=0, tiled=True)
    pieces = jnp.split(out, [sum(widths[:k]) for k in range(1, len(widths))], axis=1)
    return tuple(
        (
            jnp.moveaxis(b.reshape(-1, *t.shape[1:]), 0, dim)
            for b, t, dim in zip(pieces, turned, dims)
        )
    )


def laid_out(pieces, dim):
    pieces = jnp.moveaxis(pieces, 0, dim)
    dims = pieces.shape
    return pieces.reshape(*dims[:dim], dims[dim] * dims[dim + 1], *dims[dim + 2 :])


def all_blocks(value, axes, turns):
    pieces = value
    for k in turns:
        pieces = lax.all_gather(pieces, axes[k])
    done = turns[::-1]
    back = [done.index(k) for k in range(len(axes))]
    pieces = pieces.transpose(*back, *range(len(axes), pieces.ndim))
    return pieces.reshape(-1, *value.shape)


def gathered_by_axis(value, axes, turns, dim):
    return laid_out(all_blocks(value, axes, turns), dim)


def local(
    weight_gate,
    low_gate,
    high_gate,
    weight_up,
    low_up,
    high_up,
    weight_down,
    low_down,
    high_down,
    norm_train,
    norm_step,
):
    latest_gate = weight_gate.astype(jnp.float32) + mix_rate * jnp.dot(
        low_gate, high_gate, preferred_element_type=jnp.float32
    )
    latest_up = weight_up.astype(jnp.float32) + mix_rate * jnp.dot(
        low_up, high_up, preferred_element_type=jnp.float32
    )
    latest_down = weight_down.astype(jnp.float32) + mix_rate * jnp.dot(
        low_down, high_down, preferred_element_type=jnp.float32
    )
    narrow_gate, narrow_up, narrow_down = (
        latest_gate.astype(jnp.bfloat16),
        latest_up.astype(jnp.bfloat16),
        latest_down.astype(jnp.bfloat16),
    )
    ready_gate, ready_up, ready_down = turned_gather(
        (narrow_gate, narrow_up, narrow_down), ZERO, (0, 0, 1)
    )
    serve_norm = gathered_by_axis(
        (norm_train + norm_step).astype(jnp.bfloat16), ZERO_TP, (0, 1, 3, 2), 0
    )
    return (ready_gate, ready_up, ready_down, serve_norm)


def solution(mesh):
    finer = Mesh(
        mesh.devices.reshape(4, 4, 2, mesh.shape["tp"]), ("zero_0", "zero_1", "zero_2", "tp")
    )
    return jax.shard_map(
        local,
        mesh=finer,
        in_specs=(
            P(ZERO, "tp"),
            P(ZERO, None),
            P(None, "tp"),
            P(ZERO, "tp"),
            P(ZERO, None),
            P(None, "tp"),
            P("tp", ZERO),
            P("tp", None),
            P(None, ZERO),
            P(ZERO_TP),
            P(ZERO_TP),
        ),
        out_specs=(P(None, "tp"), P(None, "tp"), P("tp", None), P()),
        check_vma=False,
    )
```

profile of v0, /device:TPU:1, one launch (start us, length us, event | category | flops | bytes accessed | tf_op | source)
XLA Modules:
  0.0 150.4 jit_solution(1845330764220144492)
XLA Ops:
  7.2 0.0 copy-start
  7.2 0.0 all-gather.7.cloned.1.call-start
  7.2 0.7 copy-done
  8.0 1.2 fusion.3
  9.1 1.2 fusion.4
  10.4 1.2 fusion.6
  11.6 1.1 concatenate.3
  12.7 0.0 all-gather.7.cloned.1.call-update
  12.7 1.3 dynamic-slice
  14.6 0.7 add_convert_fusion
  15.3 0.2 dynamic-update-slice
  15.5 9.5 %all-reduce = bf16[40]{0:T(256)(128)(2,1)S(1)} all-reduce(bf16[40]{0:T(256)(128)(2,1)S(1)} %dynamic-update-slice), channel_id=2, replica_groups=mesh['zero_0'=4,'zero_1'=4,'zero_2'=2,'tp'=8] {'zero_0'}, use_global_device_ids=true, to_apply=%add | all-reduce | flops 40 | bytes 160
  25.0 0.1 reshape.15
  25.1 7.7 %all-gather.4 = bf16[4,4,10]{2,1,0:T(4,128)(2,1)S(1)} all-gather(bf16[1,4,10]{2,1,0:T(4,128)(2,1)S(1)} %reshape.15), channel_id=3, replica_groups=mesh['zero_0'=4,'zero_1'=4,'zero_2'=2,'tp'=8] {'zero_1'}, dimensions={0}, use_global_device_ids=true | all-gather | bytes 400 | tf_op jit(solution)/shard_map/all_gather | solution.py:35
  32.8 23.2 %all-gather.2 = bf16[32,4,10]{2,1,0:T(4,128)(2,1)S(1)} all-gather(bf16[4,4,10]{2,1,0:T(4,128)(2,1)S(1)} %all-gather.4), channel_id=4, replica_groups=mesh['zero_0'=4,'zero_1'=4,'zero_2'=2,'tp'=8] {'tp'}, dimensions={0}, use_global_device_ids=true | all-gather | bytes 2880 | tf_op jit(solution)/shard_map/all_gather | solution.py:35
  56.0 11.3 %all-gather.3 = bf16[16,4,4,10]{3,2,1,0:T(4,128)(2,1)S(1)} all-gather(bf16[8,4,4,10]{3,2,1,0:T(4,128)(2,1)S(1)} %bitcast.20), channel_id=5, replica_groups=mesh['zero_0'=4,'zero_1'=4,'zero_2'=2,'tp'=8] {'zero_2'}, dimensions={0}, use_global_device_ids=true | all-gather | bytes 7680 | tf_op jit(solution)/shard_map/all_gather | solution.py:35
  67.3 0.7 reshape_reshape.3
  68.1 31.7 %all-gather.7.cloned.1.call-done = bf16[2560,3648]{1,0:T(8,128)(2,1)} async-done(((bf16[80,3648]{1,0:T(8,128)(2,1)}), bf16[2560,3648]{1,0:T(8,128)(2,1)}) %all-gather.7.cloned.1.call-update) | async-done | bytes 18677776 | tf_op jit(solution)/shard_map/all_gather | solution.py:16
  99.7 15.8 %slice_bitcast_fusion = (bf16[1216,2560]{0,1:T(8,128)(2,1)}, bf16[2560,1216]{1,0:T(8,128)(2,1)}, bf16[2560,1216]{1,0:T(8,128)(2,1)}) fusion(bf16[2560,3648]{1,0:T(8,128)(2,1)} %all-gather.7.cloned.1.call-done), kind=kLoop, calls=%fused_computation | loop fusion | bytes 37355520 | tf_op jit(solution)/shard_map/transpose | solution.py:20
  115.5 9.3 %copy.23 = bf16[2560,1216]{0,1:T(8,128)(2,1)} copy(bf16[2560,1216]{1,0:T(8,128)(2,1)} %get-tuple-element.18) | data formatting | bytes 12451840
  124.9 9.3 %copy.24 = bf16[2560,1216]{0,1:T(8,128)(2,1)} copy(bf16[2560,1216]{1,0:T(8,128)(2,1)} %get-tuple-element.17) | data formatting | bytes 12451840
  134.2 9.3 %copy.25 = bf16[1216,2560]{1,0:T(8,128)(2,1)} copy(bf16[1216,2560]{0,1:T(8,128)(2,1)} %get-tuple-element.16) | data formatting | bytes 12451840
  (2 shorter events, 0.0 us)
Async XLA Ops:
  7.2 0.8 copy-start
  7.2 92.5 %all-gather.7.cloned.1.call-start = ((), (), s32[]{:S(2)}) async-start(), calls=%async_computation | async-start | bytes 19599360 | tf_op jit(solution)/shard_map/all_gather | solution.py:16
Sparse Core Ops, SparseCore 0:
  12.8 86.8 all-gather.6
where the time goes:
time: 151 us; the launch traced here: 150 us
  blocking collectives  51.7 us (34%)
  local copies, waits for them, and re-layouts  47.9 us (32%)
  waiting for transfers between devices  31.7 us (21%)
  between operations  14.7 us (10%)
  matrix products  3.63 us (2%)
    all_gather x3, blocking collectives, all_blocks(): pieces = lax.all_gather(pieces, axes[k])  42.2 us
    all_gather x1, waiting for transfers between devices, turned_gather(): out = lax.all_gather(both, axis, axis=0, tiled=True)  31.7 us
    unnamed x9, local copies, waits for them, and re-layouts  30.3 us
    transpose x1, local copies, waits for them, and re-layouts, turned_gather(): jnp.moveaxis(b.reshape(-1, *t.shape[1:]), 0, dim)  15.8 us
    unnamed x1, blocking collectives  9.52 us
  transfers between devices with their start and end apart: 1, of which 1 were waited for; matrix products, arithmetic and copies ran while one was open for 2% of the time, Pallas kernels for 0%

commit v1 on v0

--- a/solution.py
+++ b/solution.py
@@ -3,6 +3,7 @@
 from jax import lax
 from jax.sharding import Mesh
 from jax.sharding import PartitionSpec as P
+from jax.lax import all_to_all, axis_size
 
 ZERO = ("zero_0", "zero_1", "zero_2")
 ZERO_TP = ("zero_0", "zero_1", "zero_2", "tp")
@@ -13,7 +14,12 @@
     turned = [jnp.moveaxis(a, dim, 0) for a, dim in zip(arrays, dims)]
     widths = [t[0].size for t in turned]
     both = jnp.concatenate([t.reshape(-1, w) for t, w in zip(turned, widths)], axis=1)
-    out = lax.all_gather(both, axis, axis=0, tiled=True)
+    out = jnp.concatenate(
+        all_to_all(
+            jnp.stack(axis_size(axis) * [both]), split_axis=0, concat_axis=0, axis_name=axis
+        ),
+        0,
+    )
     pieces = jnp.split(out, [sum(widths[:k]) for k in range(1, len(widths))], axis=1)
     return tuple(
         (

time: 151 us -> 338 us (2.24); the launches traced: 150 us -> 333 us
  blocking collectives: 51.7 us -> 266 us
  waiting for transfers between devices: 31.7 us -> 0.01 us
  between operations: 14.7 us -> 1.38 us
  starting transfers between devices: 0.04 us -> 8.75 us
  local copies, waits for them, and re-layouts: 47.9 us -> 53.3 us
    unnamed x1, blocking collectives: 9.52 us -> 224 us
    all_gather x1 -> x0, waiting for transfers between devices: 31.7 us -> none  [turned_gather(): out = lax.all_gather(both, axis, axis=0, tiled=True)]
    all_to_all x0 -> x1, starting transfers between devices: none -> 8.75 us  [turned_gather(): all_to_all(jnp.stack(axis_size(axis) * [both]), split_axis=0, concat_axis...]
    another operation x0 -> x1, local copies, waits for them, and re-layouts: none -> 6.66 us  [turned_gather(): jnp.stack(axis_size(axis) * [both])]
    unnamed x9 -> x17, local copies, waits for them, and re-layouts: 30.3 us -> 29.7 us
  transfers between devices with their start and end apart: 1 -> 1, of which waited for: 1 -> 0; matrix products, arithmetic and copies ran while one was open for 2% -> 1% of each run, Pallas kernels for 0% -> 0%
where the time goes in v1:
time: 338 us; the launch traced here: 333 us
  blocking collectives  266 us (79%)
  local copies, waits for them, and re-layouts  53.3 us (16%)
  starting transfers between devices  8.75 us (3%)
  matrix products  3.63 us (1%)
    unnamed x1, blocking collectives  224 us
    all_gather x3, blocking collectives, all_blocks(): pieces = lax.all_gather(pieces, axes[k])  41.9 us
    unnamed x17, local copies, waits for them, and re-layouts  29.7 us
    transpose x1, local copies, waits for them, and re-layouts, turned_gather(): jnp.moveaxis(b.reshape(-1, *t.shape[1:]), 0, dim)  15.8 us
    all_to_all x1, starting transfers between devices, turned_gather(): all_to_all(jnp.stack(axis_size(axis) * [both]), split_axis=0, concat_axis...  8.75 us
  transfers between devices with their start and end apart: 1, of which 0 were waited for; matrix products, arithmetic and copies ran while one was open for 1% of the time, Pallas kernels for 0%

profile of v1, /device:TPU:1, one launch (start us, length us, event | category | flops | bytes accessed | tf_op | source)
XLA Modules:
  0.0 332.9 jit_solution(14690212333028656014)
XLA Ops:
  0.6 0.0 copy-start
  0.6 0.8 copy-done
  1.4 1.2 fusion.3
  2.6 1.2 fusion.4
  3.8 1.2 fusion.6
  5.1 0.4 concatenate.3
  5.4 6.7 %stack.2 = bf16[32,80,3648]{2,1,0:T(8,128)(2,1)} broadcast(bf16[80,3648]{1,0:T(8,128)(2,1)S(1)} %concatenate.3), dimensions={1,2} | broadcast | bytes 19261440 | tf_op jit(solution)/shard_map/stack | solution.py:19
  12.1 8.8 %all-to-all-start = ((bf16[32,80,3648]{2,1,0:T(8,128)(2,1)}), bf16[32,80,3648]{2,1,0:T(8,128)(2,1)}, u32[]{:S(2)}, u32[]{:S(2)}) async-start(bf16[32,80,3648]{2,1,0:T(8,128)(2,1)} %stack.2), calls=%async_computation | async-start | bytes 38010880 | tf_op jit(solution)/shard_map/all_to_all | solution.py:18
  20.9 0.0 copy-done.4
  20.9 0.6 dynamic-slice
  22.1 0.0 copy-done.2
  22.2 0.2 dynamic-update-slice
  22.4 223.9 %all-reduce = bf16[40]{0:T(256)(128)(2,1)S(1)} all-reduce(bf16[40]{0:T(256)(128)(2,1)S(1)} %dynamic-update-slice), channel_id=2, replica_groups=mesh['zero_0'=4,'zero_1'=4,'zero_2'=2,'tp'=8] {'zero_0'}, use_global_device_ids=true, to_apply=%add | all-reduce | flops 40 | bytes 160
  246.3 0.1 reshape.21
  246.4 10.7 %all-gather.4 = bf16[4,4,10]{2,1,0:T(4,128)(2,1)S(1)} all-gather(bf16[1,4,10]{2,1,0:T(4,128)(2,1)S(1)} %reshape.21), channel_id=3, replica_groups=mesh['zero_0'=4,'zero_1'=4,'zero_2'=2,'tp'=8] {'zero_1'}, dimensions={0}, use_global_device_ids=true | all-gather | bytes 400 | tf_op jit(solution)/shard_map/all_gather | solution.py:41
  257.1 22.0 %all-gather.2 = bf16[32,4,10]{2,1,0:T(4,128)(2,1)S(1)} all-gather(bf16[4,4,10]{2,1,0:T(4,128)(2,1)S(1)} %all-gather.4), channel_id=4, replica_groups=mesh['zero_0'=4,'zero_1'=4,'zero_2'=2,'tp'=8] {'tp'}, dimensions={0}, use_global_device_ids=true | all-gather | bytes 2880 | tf_op jit(solution)/shard_map/all_gather | solution.py:41
  279.1 9.2 %all-gather.3 = bf16[16,4,4,10]{3,2,1,0:T(4,128)(2,1)S(1)} all-gather(bf16[8,4,4,10]{3,2,1,0:T(4,128)(2,1)S(1)} %bitcast.21), channel_id=5, replica_groups=mesh['zero_0'=4,'zero_1'=4,'zero_2'=2,'tp'=8] {'zero_2'}, dimensions={0}, use_global_device_ids=true | all-gather | bytes 7680 | tf_op jit(solution)/shard_map/all_gather | solution.py:41
  288.3 0.7 reshape_reshape.3
  289.1 0.0 all-to-all-done
  289.1 15.8 %slice_bitcast_fusion = (bf16[1216,2560]{0,1:T(8,128)(2,1)}, bf16[2560,1216]{1,0:T(8,128)(2,1)}, bf16[2560,1216]{1,0:T(8,128)(2,1)}) fusion(bf16[2560,3648]{1,0:T(8,128)(2,1)} %bitcast.1), kind=kLoop, calls=%fused_computation | loop fusion | bytes 37355520 | tf_op jit(solution)/shard_map/transpose | solution.py:26
  304.9 9.3 %copy.21 = bf16[2560,1216]{0,1:T(8,128)(2,1)} copy(bf16[2560,1216]{1,0:T(8,128)(2,1)} %get-tuple-element.14) | data formatting | bytes 12451840
  314.2 9.3 %copy.22 = bf16[2560,1216]{0,1:T(8,128)(2,1)} copy(bf16[2560,1216]{1,0:T(8,128)(2,1)} %get-tuple-element.13) | data formatting | bytes 12451840
  323.6 9.3 %copy.23 = bf16[1216,2560]{1,0:T(8,128)(2,1)} copy(bf16[1216,2560]{0,1:T(8,128)(2,1)} %get-tuple-element.12) | data formatting | bytes 12451840
  332.9 0.0 copy-done.1
  (8 shorter events, 0.0 us)
Async XLA Ops:
  0.6 0.8 copy-start
  12.1 8.8 %copy-start.4 = (u32[256]{0:T(256)S(1)}, u32[256]{0:T(256)}, u32[]{:S(2)}) copy-start(u32[256]{0:T(256)} %constant.13) | copy-start | bytes 3076
  12.1 10.0 %copy-start.2 = (f32[10]{0:T(128)S(1)}, f32[10]{0:T(128)}, u32[]{:S(2)}) copy-start(f32[10]{0:T(128)} %param.20) | copy-start | bytes 124
  12.1 10.0 %copy-start.3 = (f32[10]{0:T(128)S(1)}, f32[10]{0:T(128)}, u32[]{:S(2)}) copy-start(f32[10]{0:T(128)} %param.21) | copy-start | bytes 124
  12.1 277.0 %all-to-all-start = ((bf16[32,80,3648]{2,1,0:T(8,128)(2,1)}), bf16[32,80,3648]{2,1,0:T(8,128)(2,1)}, u32[]{:S(2)}, u32[]{:S(2)}) async-start(bf16[32,80,3648]{2,1,0:T(8,128)(2,1)} %stack.2), calls=%async_computation | async-start | bytes 38010880 | tf_op jit(solution)/shard_map/all_to_all | solution.py:18
  314.2 18.7 %copy-start.1 = (bf16[16,1216]{1,0:T(8,128)(2,1)S(1)}, bf16[16,1216]{1,0:T(8,128)(2,1)}, u32[]{:S(2)}) copy-start(bf16[16,1216]{1,0:T(8,128)(2,1)} %param.13) | copy-start | bytes 116740
